TPU v7x, 256 devices: a whole 4x4x8 slice. The times are simulated.
256 devices in a mesh: ep: 16 (over z, core), fsdp: 4 (over x), tp: 4 (over y).
Axes of the slice: x: 4, y: 4, z: 8, core: 2. Of those that a mesh axis runs over, the one named last changes fastest.
Arguments:
- out_grad: bfloat16 [8192, 4096], P(('ep', 'fsdp')), may hold values from -1.5 to 1.5
- routes: int32 [8192, 2], P(('ep', 'fsdp')), may hold values from 0 to 15, all different within a row; in each aligned block of 128 rows (0 to 127, 128 to 255, ...) at most 32 rows name the same one
- chosen_logits: float32 [8192, 2], P(('ep', 'fsdp')), may hold values from -4 to 4
- routed_inputs: bfloat16 [16, 16, 4, 32, 4096], P('ep', None, 'fsdp'), may hold values from -6 to 6
- w_gate: bfloat16 [16, 4096, 1024], P('ep', 'fsdp', 'tp'), may hold values from -0.09375 to 0.09375
- w_up: bfloat16 [16, 4096, 1024], P('ep', 'fsdp', 'tp'), may hold values from -0.09375 to 0.09375
- w_down: bfloat16 [16, 1024, 4096], P('ep', 'tp', 'fsdp'), may hold values from -0.1875 to 0.1875
Outputs:
- input_grad: bfloat16 [8192, 4096], P(('ep', 'fsdp'))
- logit_grad: float32 [8192, 2], P(('ep', 'fsdp'))
- grad_gate: float32 [16, 4096, 1024], P('ep', 'fsdp', 'tp')
- grad_up: float32 [16, 4096, 1024], P('ep', 'fsdp', 'tp')
- grad_down: float32 [16, 1024, 4096], P('ep', 'tp', 'fsdp')
Inputs may be any that keep to these rules, and one draw needn't show every extreme that they name: Each row of routes names 2 different experts. In each token group of 128 consecutive rows no expert is named by more than 32 rows, a bound that some block reaches.
All inputs are finite; a program needn't handle non-finite values.
Results may differ from a plain program's by a relative error of at most 0.015.
Values may be sent and summed in bfloat16 or wider, within the bound.
No kernel may reach another device: no remote copies, remote signals or barrier semaphores. Data moves between devices by JAX's collectives and lax.ppermute only.
A program may use at most 128 MiB of HBM per device.

v0:
```python
import functools

import jax
import jax.numpy as jnp
from jax import lax
from jax.experimental import pallas as pl
from jax.experimental.pallas import tpu as pltpu
from jax.sharding import PartitionSpec as P


RING = 4
LANES = 128
MIB = 1 << 20


SHIFTS = (0, 1, -1, 2, -2, 3, -3, 4)
GROUPS = ((0, 1, 2, 3, 4), (5, 6, 7))


def shift(x, axis, step):
    n = lax.axis_size(axis)
    return lax.ppermute(x, axis, [(i, (i + step) % n) for i in range(n)])


def shift_z(x, step):
    n = lax.axis_size("ep")
    return lax.ppermute(x, "ep", [(i, (i + 2 * step) % n) for i in range(n)])


def swap_cores(x):
    return lax.ppermute(x, "ep", [(i, i ^ 1) for i in range(lax.axis_size("ep"))])


def ring_gather(block, axis):
    half = block.shape[0] // 2
    prev = shift(block, axis, 1)
    following = shift(block, axis, -1)
    far_top = shift(prev[:half], axis, 1)
    far_bottom = shift(following[half:], axis, -1)
    return block, following, far_top, far_bottom, prev


def far_halves(top, bottom, axis):
    return shift(top, axis, 1), shift(bottom, axis, -1)


def neighbours(following, prev, axis):
    return shift(following, axis, 1), shift(prev, axis, -1)


def call(kernel, out_shape, mib=8, **options):
    return pl.pallas_call(
        kernel,
        out_shape=out_shape,
        compiler_params=pltpu.CompilerParams(vmem_limit_bytes=mib * MIB),
        **options,
    )


def bf16(*shape):
    return jax.ShapeDtypeStruct(shape, jnp.bfloat16)


def f32(*shape):
    return jax.ShapeDtypeStruct(shape, jnp.float32)


def dot(left, right, left_dim=1, right_dim=0):
    return lax.dot_general(
        left, right, (((left_dim,), (right_dim,)), ((), ())), preferred_element_type=jnp.float32
    )


def add_half(whole, half, index, start=0):
    rows, columns = whole.shape
    rows //= 2
    blocks = max(rows // 512, 1)
    rows //= blocks

    def kernel(whole_ref, half_ref, out_ref):
        first = pl.multiple_of(start + pl.program_id(0) * rows, 16)
        total = whole_ref[...].astype(jnp.float32)
        total += half_ref[pl.ds(first, rows)].astype(jnp.float32)
        out_ref[...] = total.astype(jnp.bfloat16)

    spec = pl.BlockSpec((rows, columns), lambda i: (index * blocks + i, 0))
    return call(
        kernel,
        bf16(*whole.shape),
        grid=(blocks,),
        in_specs=[spec, pl.BlockSpec(memory_space=pltpu.VMEM)],
        out_specs=spec,
        input_output_aliases={0: 0},
    )(whole, half)


def pack(w_gate, w_up, w_down):
    depth, width = w_gate.shape

    def kernel(gate_ref, up_ref, down_ref, out_ref):
        out_ref[:depth] = gate_ref[...]
        out_ref[depth : 2 * depth] = up_ref[...]
        out_ref[2 * depth :] = down_ref[...].T

    return call(kernel, bf16(3 * depth, width))(
        *(pltpu.with_memory_space_constraint(w, pltpu.HBM) for w in (w_gate, w_up, w_down))
    )


def weight_parts(refs, r, depth):
    half = depth // 2
    if r == 2:
        top, bottom = refs[2], refs[3]
        return [(top, 0, depth)], [(top, depth, half), (bottom, 0, half)], [(bottom, half, depth)]
    ref = refs[(0, 1, None, 4)[r]]
    return tuple([(ref, i * depth, depth)] for i in range(3))


def start_select(refs, r, out_ref, sem, depth):
    for k in range(RING):

        @pl.when(r == k)
        def _():
            if k == 2:
                rows = 3 * depth // 2
                pieces = [(refs[2], 0, rows), (refs[3], rows, 2 * depth - rows)]
            else:
                pieces = [(refs[(0, 1, None, 4)[k]], 0, 2 * depth)]
            for ref, first, count in pieces:
                source = ref.at[pl.ds(0, count)]
                pltpu.make_async_copy(source, out_ref.at[pl.ds(first, count)], sem).start()


def wait_select(out_ref, sem):
    pltpu.make_async_copy(out_ref, out_ref, sem).wait()


def fill_rows(here_ref, x_ref, rows_ref):
    capacity = x_ref.shape[3]
    z, core = here_ref[2], here_ref[3]
    count = len(SHIFTS)
    for j, step in enumerate(SHIFTS):
        for k in range(2):
            source = ((z - step + count) % count) * 2 + (core if k == 0 else 1 - core)
            rows_ref[pl.ds((2 * j + k) * capacity, capacity)] = x_ref[0, source, 0]


def activations(here, routed_inputs, weights, width):
    _, sources, _, capacity, model_width = routed_inputs.shape
    depth = model_width // RING
    slots = sources * capacity

    def kernel(here_ref, x_ref, *refs):
        weight_refs, (hidden_ref, silu_ref, slope_ref) = refs[:5], refs[5:8]
        x, total, chosen, sems = refs[8:]
        step = pl.program_id(0)
        now = step % 2

        def start(r):
            start_select(weight_refs, r, chosen.at[r % 2], sems.at[r % 2], depth)

        @pl.when(step == 0)
        def _():
            start(step)

        @pl.when(step < RING - 1)
        def _():
            start(step + 1)

        @pl.when(step == 0)
        def _():
            total[...] = jnp.zeros_like(total)

        fill_rows(here_ref, x_ref, x)
        wait_select(chosen.at[now], sems.at[now])

        def add(k, carry):
            rows = pl.ds(pl.multiple_of(k * depth, depth), depth)
            total[k] += dot(x[...], chosen[now, rows])
            return carry

        lax.fori_loop(0, 2, add, 0)

        @pl.when(step == RING - 1)
        def _():
            def finish(i, carry):
                rows = pl.ds(pl.multiple_of(i * LANES, LANES), LANES)
                gate_act, up_act = total[0, rows], total[1, rows]
                sigmoid_gate = jax.nn.sigmoid(gate_act)
                silu_gate = gate_act * sigmoid_gate
                hidden_ref[rows] = (silu_gate * up_act).astype(jnp.bfloat16)
                silu_ref[rows] = silu_gate
                slope_ref[rows] = up_act * sigmoid_gate * (1.0 + gate_act * (1.0 - sigmoid_gate))
                return carry

            lax.fori_loop(0, slots // LANES, finish, 0)

    whole = pl.BlockSpec(memory_space=pltpu.VMEM)
    return call(
        kernel,
        (bf16(slots, width), f32(slots, width), f32(slots, width)),
        mib=18,
        grid_spec=pltpu.PrefetchScalarGridSpec(
            num_scalar_prefetch=1,
            grid=(RING,),
            in_specs=[
                pl.BlockSpec(
                    (1, sources, 1, capacity, depth),
                    lambda i, here: (0, 0, 0, 0, (here[0] + i) % RING),
                )
            ]
            + [whole] * 5,
            out_specs=(pl.BlockSpec((slots, width), lambda i, here: (0, 0)),) * 3,
            scratch_shapes=[pltpu.VMEM((slots, depth), jnp.bfloat16)]
            + [pltpu.VMEM((2, slots, width), jnp.float32)]
            + [pltpu.VMEM((2, 2 * depth, width), jnp.bfloat16), pltpu.SemaphoreType.DMA((2,))],
        ),
    )(here, routed_inputs, *weights)


def pair_gradients(here, arrays, places, weights, hidden, silu, slope, groups):
    slots, width = hidden.shape
    depth = arrays[0].shape[1]
    spans, at = [], 0
    for rows in groups:
        spans.append((at, rows))
        at += rows

    def kernel(here_ref, *refs):
        scaled_refs, refs = refs[: len(arrays)], refs[len(arrays) :]
        weight_refs, (hidden_ref, silu_ref, slope_ref) = refs[:5], refs[5:8]
        pair_ref, extra_ref, by_r, top_ref, bottom_ref = refs[8:13]
        chosen, downs, hidden_grad_ref, chosen_sem, sems = refs[13:]
        t = here_ref[1]
        for array, first, q, slot, count in places:
            r = (t + q) % RING
            source = scaled_refs[array].at[pl.ds(first, count)]
            pltpu.make_async_copy(source, by_r.at[r, pl.ds(slot, count)], sems.at[0, r]).start()
        for r in range(RING):
            ((ref, first, count),) = weight_parts(weight_refs, r, depth)[2]
            pltpu.make_async_copy(ref.at[pl.ds(first, count)], downs.at[r], sems.at[1, r]).start()
        start_select(weight_refs, (t + 2) % RING, chosen, chosen_sem, depth)
        hidden_grad_ref[...] = jnp.zeros_like(hidden_grad_ref)

        def add_columns(r, carry):
            pltpu.make_async_copy(by_r.at[r], by_r.at[r], sems.at[0, r]).wait()
            pltpu.make_async_copy(downs.at[r], downs.at[r], sems.at[1, r]).wait()
            hidden_grad_ref[...] += dot(by_r[r], downs[r])
            return carry

        lax.fori_loop(0, RING, add_columns, 0)

        def finish(i, carry):
            rows = pl.ds(pl.multiple_of(i * LANES, LANES), LANES)
            hidden_grad = hidden_grad_ref[rows]
            products = jnp.sum(
                hidden_grad * hidden_ref[rows].astype(jnp.float32), axis=1, keepdims=True
            )
            high = products.astype(jnp.bfloat16).astype(jnp.float32)
            lane = lax.broadcasted_iota(jnp.int32, (LANES, LANES), 1)
            extra = jnp.where(lane == 0, high, jnp.where(lane == 1, products - high, 0.0))
            extra_ref[rows] = extra.astype(jnp.bfloat16)
            pair_ref[rows, :width] = (hidden_grad * slope_ref[rows]).astype(jnp.bfloat16)
            pair_ref[rows, width:] = (hidden_grad * silu_ref[rows]).astype(jnp.bfloat16)
            return carry

        lax.fori_loop(0, slots // LANES, finish, 0)
        wait_select(chosen, chosen_sem)

        def put(columns, value):
            for start, rows in spans:
                middle = start + rows // 2
                half = pl.ds(start // 2, rows // 2)
                top_ref[half, columns] = value[start:middle]
                bottom_ref[half, columns] = value[middle : start + rows]

        slot_part(pair_ref, chosen, depth, put)

    anywhere = pl.BlockSpec(memory_space=pl.ANY)
    whole = pl.BlockSpec(memory_space=pltpu.VMEM)
    outs = [bf16(slots, 2 * width), bf16(slots, LANES), bf16(RING, slots, depth)]
    outs += [bf16(slots // 2, depth)] * 2
    return call(
        kernel,
        tuple(outs),
        mib=24,
        grid_spec=pltpu.PrefetchScalarGridSpec(
            num_scalar_prefetch=1,
            grid=(1,),
            in_specs=[anywhere] * len(arrays) + [whole] * 8,
            out_specs=(whole,) * len(outs),
            scratch_shapes=[
                pltpu.VMEM((2 * depth, width), jnp.bfloat16),
                pltpu.VMEM((RING, depth, width), jnp.bfloat16),
                pltpu.VMEM((slots, width), jnp.float32),
                pltpu.SemaphoreType.DMA,
                pltpu.SemaphoreType.DMA((2, RING)),
            ],
        ),
    )(here, *arrays, *weights, hidden, silu, slope)


def slot_part(pair_ref, weights, depth, put):
    half = depth // 2
    width = pair_ref.shape[1] // 2

    def columns(i, carry):
        at = pl.multiple_of(i * half, half)
        value = dot(pair_ref[:, :width], weights[pl.ds(at, half)], 1, 1)
        value += dot(pair_ref[:, width:], weights[pl.ds(depth + at, half)], 1, 1)
        put(pl.ds(at, half), value.astype(jnp.bfloat16))
        return carry

    lax.fori_loop(0, 2, columns, 0)


def slot_gradients(here, pair, weights, groups):
    slots = pair.shape[0]
    width = pair.shape[1] // 2
    depth = weights[0].shape[0] // 3
    spans, at = [], 0
    for rows in groups:
        spans.append(slice(at, at + rows))
        at += rows

    def kernel(here_ref, pair_ref, *refs):
        weight_refs, out_refs, (parts, chosen, sems) = refs[:5], refs[5:-3], refs[-3:]
        t, step = here_ref[1], pl.program_id(0)

        def start(i):
            q = i + i // 2
            start_select(weight_refs, (t + q) % RING, chosen.at[i % 2], sems.at[i % 2], depth)

        @pl.when(step == 0)
        def _():
            start(0)
            start(1)

        now = step % 2
        wait_select(chosen.at[now], sems.at[now])

        def put(columns, value):
            parts[step, :, columns] = value

        slot_part(pair_ref, chosen.at[now], depth, put)

        @pl.when(step == 0)
        def _():
            start(2)

        @pl.when(step == 2)
        def _():
            for i, span in enumerate(spans):
                for j in range(3):

                    def copy_rows(k, carry):
                        at = pl.multiple_of(k * 64, 64)
                        out_refs[3 * i + j][pl.ds(at, 64)] = parts[j, pl.ds(span.start + at, 64)]
                        return carry

                    lax.fori_loop(0, (span.stop - span.start) // 64, copy_rows, 0)

    whole = pl.BlockSpec(memory_space=pltpu.VMEM)
    outs = tuple(bf16(rows, depth) for rows in groups for _ in range(3))
    parts = call(
        kernel,
        outs,
        mib=17,
        grid_spec=pltpu.PrefetchScalarGridSpec(
            num_scalar_prefetch=1,
            grid=(3,),
            in_specs=[whole] * 6,
            out_specs=(whole,) * len(outs),
            scratch_shapes=[
                pltpu.VMEM((3, slots, depth), jnp.bfloat16),
                pltpu.VMEM((2, 2 * depth, width), jnp.bfloat16),
                pltpu.SemaphoreType.DMA((2,)),
            ],
        ),
    )(here, pair, *weights)
    return [parts[3 * i : 3 * i + 3] for i in range(len(groups))]


def weight_chunk(here, distances, routed_inputs, hidden, pair, scaled, received=None):
    _, sources, _, capacity, model_width = routed_inputs.shape
    depth = model_width // RING
    slots, width = hidden.shape
    half = depth // 2
    received = received or ()
    near = len(distances) == 2

    def distance(i):
        return distances[0] + 2 * i if near else distances[0]

    def kernel(here_ref, x_ref, hidden_ref, pair_ref, scaled_ref, *refs):
        x, refs = refs[-1], refs[:-1]
        fill_rows(here_ref, x_ref, x)

        def put(at, value):
            place = pl.ds(at, value.shape[0])
            if received:
                value += refs[0][place].astype(jnp.float32) + refs[1][place].astype(jnp.float32)
                for i in range(2):

                    @pl.when((at >= i * depth) & (at < (i + 1) * depth))
                    def _():
                        refs[2 + i][pl.ds(at - i * depth, value.shape[0])] = value

                return value
            if near:
                for i in range(2):

                    @pl.when(pl.program_id(0) == i)
                    def _():
                        refs[i][place] = value.astype(jnp.bfloat16)

                return value
            for i in range(2):

                @pl.when((at >= 3 * i * half) & (at < 3 * (i + 1) * half))
                def _():
                    start = at - 3 * i * half
                    refs[i][pl.ds(start, value.shape[0])] = value.astype(jnp.bfloat16)

            return value

        def inputs_part(i, carry):
            columns = pl.ds(pl.multiple_of((i % 2) * half, half), half)
            lanes = pl.ds(pl.multiple_of((i // 2) * width, width), width)
            put(pl.multiple_of(i * half, half), dot(x[:, columns], pair_ref[:, lanes], 0, 0))
            return carry

        def down_part(c, carry):
            lanes = pl.ds(pl.multiple_of(c * width, width), width)
            value = dot(hidden_ref[...], scaled_ref[0, :, lanes], 0, 0)
            at = pl.multiple_of(2 * depth + c * width, width)
            value = put(at, value)
            if received:
                refs[4][:, lanes] = value
            return carry

        lax.fori_loop(0, 4, inputs_part, 0)
        lax.fori_loop(0, depth // width, down_part, 0)

    whole = pl.BlockSpec(memory_space=pltpu.VMEM)
    if received:
        outs = (f32(depth, width), f32(depth, width), f32(width, depth))
    elif near:
        outs = (bf16(6 * half, width),) * 2
    else:
        outs = (bf16(3 * half, width),) * 2
    return call(
        kernel,
        outs,
        mib=18 if received else 14,
        grid_spec=pltpu.PrefetchScalarGridSpec(
            num_scalar_prefetch=1,
            grid=(len(distances),),
            in_specs=[
                pl.BlockSpec(
                    (1, sources, 1, capacity, depth),
                    lambda i, here: (0, 0, 0, 0, (here[0] + distance(i)) % RING),
                ),
                whole,
                whole,
                pl.BlockSpec((1, slots, depth), lambda i, here: (distance(i), 0, 0)),
            ]
            + [whole] * len(received),
            out_specs=(whole,) * len(outs),
            scratch_shapes=[pltpu.VMEM((slots, depth), jnp.bfloat16)],
        ),
    )(here, routed_inputs, hidden, pair, scaled, *received)


def join(outs):
    arrays = []
    for out in outs:
        for array, _, _ in out:
            if not any(array is a for a in arrays):
                arrays.append(array)
    index = {id(a): i for i, a in enumerate(arrays)}

    def kernel(*refs):
        for out, out_ref in zip(outs, refs[len(arrays) :]):
            at = 0
            for array, first, rows in out:
                out_ref[pl.ds(at, rows)] = refs[index[id(array)]][first : first + rows]
                at += rows

    columns = arrays[0].shape[1]
    shapes = tuple(bf16(sum(rows for _, _, rows in out), columns) for out in outs)
    return call(kernel, shapes)(*arrays)


def messages(own, other):
    count = len(SHIFTS)
    rows, columns = own.shape
    rows //= count

    def kernel(own_ref, other_ref, *out_refs):
        for j, out_ref in enumerate(out_refs):
            out_ref[:rows] = own_ref[j * rows : (j + 1) * rows]
            out_ref[rows:] = other_ref[j * rows : (j + 1) * rows]

    return call(kernel, (bf16(2 * rows, columns),) * count)(own, other)


def unpack_messages(blocks):
    rows, columns = blocks[0].shape
    rows //= 2

    def kernel(*refs):
        own_ref, other_ref = refs[-2:]
        for j, ref in enumerate(refs[:-2]):
            own_ref[pl.ds(j * rows, rows)] = ref[:rows]
            other_ref[pl.ds(j * rows, rows)] = ref[rows:]

    return call(kernel, (bf16(len(blocks) * rows, columns),) * 2)(*blocks)


def leaving_rows(own, from_prev, from_next, extra, start, count):
    rows, narrow = own.shape
    rows //= count

    def kernel(own_ref, prev_ref, next_ref, extra_ref, *out_refs):
        for j, out_ref in enumerate(out_refs):
            span = slice(j * rows, (j + 1) * rows)
            total = own_ref[span].astype(jnp.float32) + prev_ref[span].astype(jnp.float32)
            total += next_ref[span].astype(jnp.float32)
            out_ref[:, :narrow] = total.astype(jnp.bfloat16)
            out_ref[:, narrow:] = extra_ref[start + j * rows : start + (j + 1) * rows]

    outs = (bf16(rows, narrow + LANES),) * count
    return call(kernel, outs)(own, from_prev, from_next, extra)


def token_rows(slot_index, back):
    tokens = slot_index.shape[0]
    rows, wide = back[0].shape
    narrow = wide - LANES

    def kernel(slot_ref, *refs):
        out_ref = refs[-1]
        total = jnp.zeros((tokens, narrow), jnp.float32)
        chosen = [jnp.zeros((tokens, LANES), jnp.float32)] * 2
        for h, back_ref in enumerate(refs[:-1]):
            slot = lax.broadcasted_iota(jnp.int32, (tokens, rows), 1) + h * rows
            picks = [
                jnp.where(slot_ref[:, k : k + 1] == slot, 1.0, 0.0).astype(jnp.bfloat16)
                for k in range(2)
            ]
            total += dot(picks[0] + picks[1], back_ref[:, :narrow])
            chosen = [c + dot(p, back_ref[:, narrow:]) for c, p in zip(chosen, picks)]
        out_ref[:, :narrow] = total.astype(jnp.bfloat16)
        lane = lax.broadcasted_iota(jnp.int32, (tokens, LANES), 1)
        tail = jnp.zeros((tokens, LANES), jnp.float32)
        for k in range(2):
            value = chosen[k][:, 0:1] + chosen[k][:, 1:2]
            high = value.astype(jnp.bfloat16).astype(jnp.float32)
            tail = jnp.where(lane == 2 * k, high, jnp.where(lane == 2 * k + 1, value - high, tail))
        out_ref[:, narrow:] = tail.astype(jnp.bfloat16)

    return call(kernel, bf16(tokens, wide))(slot_index, *back)


def finish_tokens(here, gate_probs, gathered):
    tokens, wide = gathered[0].shape
    narrow = wide - LANES

    def kernel(here_ref, probs_ref, *refs):
        out_ref, logit_ref = refs[RING:]
        total = jnp.zeros((tokens, LANES), jnp.float32)
        for q in range(RING):
            first = ((here_ref[0] + here_ref[1] + q) % RING) * narrow
            out_ref[:, pl.ds(pl.multiple_of(first, LANES), narrow)] = refs[q][:, :narrow]
            total += refs[q][:, narrow:].astype(jnp.float32)
        chosen = [
            (total[:, 2 * k : 2 * k + 1] + total[:, 2 * k + 1 : 2 * k + 2])
            .astype(jnp.bfloat16)
            .astype(jnp.float32)
            for k in range(2)
        ]
        both = chosen[0] + chosen[1]
        for k in range(2):
            logit_ref[:, k : k + 1] = chosen[k] - probs_ref[:, k : k + 1] * both

    whole = pl.BlockSpec(memory_space=pltpu.VMEM)
    return call(
        kernel,
        (bf16(tokens, RING * narrow), f32(tokens, 2)),
        grid_spec=pltpu.PrefetchScalarGridSpec(
            num_scalar_prefetch=1,
            grid=(1,),
            in_specs=[whole] * (RING + 1),
            out_specs=(whole,) * 2,
        ),
    )(here, gate_probs, *gathered)


def slots_of(routes, z, core, capacity, experts):
    tokens = routes.shape[0]
    hot = (routes[:, :, None] == jnp.arange(experts, dtype=jnp.int32)).astype(jnp.bfloat16)
    before = jnp.arange(tokens)[:, None] > jnp.arange(tokens)[None, :]
    earlier = dot(before.astype(jnp.bfloat16), hot[:, 0] + hot[:, 1])
    place = jnp.sum(earlier[:, None, :] * hot.astype(jnp.float32), axis=2).astype(jnp.int32)
    count = len(SHIFTS)
    distance = (routes // 2 - z + count) % count
    index = jnp.where(
        distance <= count // 2, jnp.maximum(2 * distance - 1, 0), 2 * (count - distance)
    )
    other = (routes % 2 != core).astype(jnp.int32)
    return (other * count + index) * capacity + place


def layer(out_grad, routes, chosen_logits, routed_inputs, w_gate, w_up, w_down):
    experts = lax.axis_size("ep")
    f, t = lax.axis_index("fsdp"), lax.axis_index("tp")
    z, core = lax.axis_index("ep") // 2, lax.axis_index("ep") % 2
    here = jnp.stack([f, t, z, core]).astype(jnp.int32)
    model_width = out_grad.shape[1]
    capacity = routed_inputs.shape[3]
    slots = experts * capacity
    narrow = model_width // RING
    width = w_gate.shape[2]
    block = 2 * capacity

    weights = ring_gather(pack(w_gate[0], w_up[0], w_down[0]), "fsdp")

    gate_probs = jax.nn.softmax(chosen_logits, axis=-1)
    slot_index = slots_of(routes, z, core, capacity, experts)
    piece = lax.dynamic_slice_in_dim(out_grad, ((f + t) % RING) * narrow, narrow, 1)
    weighted = gate_probs[:, :, None] * piece.astype(jnp.float32)[:, None, :]
    weighted = weighted.astype(jnp.bfloat16)

    def routed(first):
        slot = first + jnp.arange(slots // 2, dtype=jnp.int32)
        picks = (slot_index[:, :, None] == slot).astype(jnp.bfloat16)
        return lax.dot_general(
            picks, weighted, (((0, 1), (0, 1)), ((), ())), preferred_element_type=jnp.float32
        ).astype(jnp.bfloat16)

    own, other = routed(0), swap_cores(routed(slots // 2))
    sent = messages(own, other)
    arrived = [sent[0]] + [shift_z(sent[j], SHIFTS[j]) for j in range(1, len(SHIFTS))]
    groups = [len(group) * block for group in GROUPS]
    count0, count1 = groups
    half = count0 // 2
    own0 = join([[(arrived[j], 0, block) for j in GROUPS[0]]])[0]
    prev0, next0 = shift(own0, "tp", 1), shift(own0, "tp", -1)
    pieces = [(arrived[j], 0, block) for j in GROUPS[1]]
    own1, prev1, next1 = join(
        [pieces, pieces + [(prev0, 0, half)], pieces + [(next0, half, half)]]
    )
    prev1, next1 = shift(prev1, "tp", 1), shift(next1, "tp", -1)
    far1 = shift(own1, "tp", 2)
    arrays = [own0, next0, prev0, own1, next1, prev1, far1]
    places = [(0, 0, 0, 0, count0), (1, 0, 1, 0, count0), (2, 0, 3, 0, count0)]
    places += [(3, 0, 0, count0, count1), (4, 0, 1, count0, count1), (5, 0, 3, count0, count1)]
    places += [(5, count1, 2, 0, half), (4, count1, 2, half, half), (6, 0, 2, count0, count1)]

    hidden, silu, slope = activations(here, routed_inputs, weights, width)
    pair, extra, scaled, *far = pair_gradients(
        here, arrays, places, weights, hidden, silu, slope, groups
    )
    far = far_halves(*far, "tp")
    parts = slot_gradients(here, pair, weights, groups)
    leaving = []
    for g, group in enumerate(GROUPS):
        own, following, prev = parts[g]
        start = group[0] * block
        following = add_half(following, far[0], 0, start // 2)
        prev = add_half(prev, far[1], 1, start // 2)
        received = neighbours(following, prev, "tp")
        leaving += leaving_rows(own, *received, extra, start, len(group))

    chunk = functools.partial(
        weight_chunk, here, routed_inputs=routed_inputs, hidden=hidden, pair=pair, scaled=scaled
    )
    far = far_halves(*chunk((2,)), "fsdp")
    following, prev = chunk((1, 3))
    received = neighbours(add_half(following, far[0], 0), add_half(prev, far[1], 1), "fsdp")
    grad_gate, grad_up, grad_down = chunk((0,), received=received)

    returned = [leaving[0]] + [shift_z(leaving[j], -SHIFTS[j]) for j in range(1, len(SHIFTS))]
    own, other = unpack_messages(returned)
    mine = token_rows(slot_index, [own, swap_cores(other)])
    tokens_by_ring = [mine] + [shift(mine, "tp", -q) for q in range(1, RING)]
    input_grad, logit_grad = finish_tokens(here, gate_probs, tokens_by_ring)
    return input_grad, logit_grad, grad_gate[None], grad_up[None], grad_down[None]


def solution(mesh):
    return jax.shard_map(
        layer,
        mesh=mesh,
        in_specs=(
            P(("ep", "fsdp"), None),
            P(("ep", "fsdp"), None),
            P(("ep", "fsdp"), None),
            P("ep", None, "fsdp", None, None),
            P("ep", "fsdp", "tp"),
            P("ep", "fsdp", "tp"),
            P("ep", "tp", "fsdp"),
        ),
        out_specs=(
            P(("ep", "fsdp"), None),
            P(("ep", "fsdp"), None),
            P("ep", "fsdp", "tp"),
            P("ep", "fsdp", "tp"),
            P("ep", "tp", "fsdp"),
        ),
        check_vma=False,
    )
```

profile of v0, /device:TPU:1, one launch (start us, length us, event | category | flops | bytes accessed | tf_op | source)
XLA Modules:
  0.0 203.1 jit_solution(17738292562555633839)
XLA Ops:
  9.9 3.1 %collective-permute-start = (bf16[256,1024]{1,0:T(8,128)(2,1)S(1)}, bf16[256,1024]{1,0:T(8,128)(2,1)S(1)}, u32[]{:S(2)}, u32[]{:S(2)}) collective-permute-start(bf16[256,1024]{1,0:T(8,128)(2,1)S(1)} %fusion.1), channel_id=1, source_target_pairs={{0,16},{16,0},{32,48},{48,32},{64,80},{80,64},{96,112},{112,96},{1... | collective-permute-start | bytes 1572872 | tf_op jit(solution)/shard_map/ppermute | solution.py:31
  14.7 3.9 %collective-permute-start.2 = (bf16[64,1024]{1,0:T(8,128)(2,1)S(1)}, bf16[64,1024]{1,0:T(8,128)(2,1)S(1)}, u32[]{:S(2)}, u32[]{:S(2)}) collective-permute-start(bf16[64,1024]{1,0:T(8,128)(2,1)S(1)} %get-tuple-element.51), channel_id=1, source_target_pairs={{0,224},{16,240},{32,0},{48,16},{64,32},{80,48},{96,64},{112,80},{... | collective-permute-start | bytes 393224 | tf_op jit(solution)/shard_map/ppermute | solution.py:27
  18.7 3.4 %collective-permute-done.1.refs_1_ = bf16[64,1024]{1,0:T(8,128)(2,1)S(1)} collective-permute-done((bf16[64,1024]{1,0:T(8,128)(2,1)S(1)}, bf16[64,1024]{1,0:T(8,128)(2,1)S(1)}, u32[]{:S(2)}, u32[]{:S(2)}) %collective-permute-start.1) | collective-permute-done | bytes 131104 | tf_op jit(solution)/shard_map/ppermute | solution.py:27
  23.8 4.0 %collective-permute-done.3.refs_3_ = bf16[64,1024]{1,0:T(8,128)(2,1)S(1)} collective-permute-done((bf16[64,1024]{1,0:T(8,128)(2,1)S(1)}, bf16[64,1024]{1,0:T(8,128)(2,1)S(1)}, u32[]{:S(2)}, u32[]{:S(2)}) %collective-permute-start.3) | collective-permute-done | bytes 131104 | tf_op jit(solution)/shard_map/ppermute | solution.py:27
  32.3 5.3 %collective-permute-done.14.refs_4_.refs_11_ = bf16[3072,256]{1,0:T(8,128)(2,1)S(1)} collective-permute-done((bf16[3072,256]{1,0:T(8,128)(2,1)S(1)}, bf16[3072,256]{1,0:T(8,128)(2,1)S(1)}, u32[]{:S(2)}, u32[]{:S(2)}) %collective-permute-start.14) | collective-permute-done | bytes 1572896 | tf_op jit(solution)/shard_map/ppermute | solution.py:22
  37.6 8.6 %collective-permute-start.8 = (bf16[64,1024]{1,0:T(8,128)(2,1)S(1)}, bf16[64,1024]{1,0:T(8,128)(2,1)S(1)}, u32[]{:S(2)}, u32[]{:S(2)}) collective-permute-start(bf16[64,1024]{1,0:T(8,128)(2,1)S(1)} %get-tuple-element.55), channel_id=1, source_target_pairs={{0,160},{16,176},{32,192},{48,208},{64,224},{80,240},{96,0},{112,1... | collective-permute-start | bytes 393224 | tf_op jit(solution)/shard_map/ppermute | solution.py:27
  49.1 10.9 %collective-permute-done.8.refs_1_ = bf16[64,1024]{1,0:T(8,128)(2,1)S(1)} collective-permute-done((bf16[64,1024]{1,0:T(8,128)(2,1)S(1)}, bf16[64,1024]{1,0:T(8,128)(2,1)S(1)}, u32[]{:S(2)}, u32[]{:S(2)}) %collective-permute-start.8) | collective-permute-done | bytes 131104 | tf_op jit(solution)/shard_map/ppermute | solution.py:27
  61.6 3.0 %collective-permute-start.10 = (bf16[352,1024]{1,0:T(8,128)(2,1)S(1)}, bf16[352,1024]{1,0:T(8,128)(2,1)S(1)}, u32[]{:S(2)}, u32[]{:S(2)}) collective-permute-start(bf16[352,1024]{1,0:T(8,128)(2,1)S(1)} %get-tuple-element.58), channel_id=1, source_target_pairs={{0,3},{1,0},{2,1},{3,2},{4,7},{5,4},{6,5},{7,6},{8,11},{9,8},{10,9... | collective-permute-start | bytes 2162696 | tf_op jit(solution)/shard_map/ppermute | solution.py:22
  66.5 11.5 %collective-permute-done.16.refs_3_.refs_10_ = bf16[1536,256]{1,0:T(8,128)(2,1)S(1)} collective-permute-done((bf16[1536,256]{1,0:T(8,128)(2,1)S(1)}, bf16[1536,256]{1,0:T(8,128)(2,1)S(1)}, u32[]{:S(2)}, u32[]{:S(2)}) %collective-permute-start.16) | collective-permute-done | bytes 786464 | tf_op jit(solution)/shard_map/ppermute | solution.py:22
  78.0 6.9 %shard_map.114 = (bf16[512,256]{1,0:T(8,128)(2,1)S(1)}, f32[512,256]{1,0:T(8,128)S(1)}, f32[512,256]{1,0:T(8,128)S(1)}) custom-call(s32[4]{0:T(128)S(1)} %pad_add_fusion.here_ref, bf16[1,16,1,32,4096]{4,3,2,1,0:T(8,128)(2,1)S(1)} %copy-done, bf16[3072,256]{1,0:T(8,128)(2,1)S(1)} %shard_map.113.refs_0_.refs_7_, ...), custom_call_target="tpu_custom_call" | custom-call | tf_op jit(solution)/shard_map/pallas_call | solution.py:199
  84.9 4.6 %collective-permute-done.12.refs_6_ = bf16[192,1024]{1,0:T(8,128)(2,1)S(1)} collective-permute-done((bf16[192,1024]{1,0:T(8,128)(2,1)S(1)}, bf16[192,1024]{1,0:T(8,128)(2,1)S(1)}, u32[]{:S(2)}, u32[]{:S(2)}) %collective-permute-start.12) | collective-permute-done | bytes 393248 | tf_op jit(solution)/shard_map/ppermute | solution.py:22
  89.5 7.2 %shard_map.115 = (bf16[512,512]{1,0:T(8,128)(2,1)S(1)}, bf16[512,128]{1,0:T(8,128)(2,1)S(1)}, bf16[4,512,1024]{2,1,0:T(8,128)(2,1)S(1)}, bf16[256,1024]{1,0:T(8,128)(2,1)S(1)}, bf16[256,1024]{1,0:T(8,128)(2,1)S(1)}) custom-call(s32[4]{0:T(128)S(1)} %pad_add_fusion.here_ref, bf16[320,1024]{1,0:T(8,128)(2,1)S(1)} %shard_map.111.refs_0_, ...), custom_call_target="tpu_custom_call" | custom-call | tf_op jit(solution)/shard_map/pallas_call | solution.py:283
  96.7 3.5 %shard_map.127 = (bf16[1536,256]{1,0:T(8,128)(2,1)S(1)}, bf16[1536,256]{1,0:T(8,128)(2,1)S(1)}) custom-call(s32[4]{0:T(128)S(1)} %pad_add_fusion.here_ref, bf16[1,16,1,32,4096]{4,3,2,1,0:T(8,128)(2,1)S(1)} %copy-done, bf16[512,256]{1,0:T(8,128)(2,1)S(1)} %get-tuple-element.60.refs_12_.hidden_ref, bf16[512,512]{1,0:T(8,128)(2,1)S(1)} %get-tuple-element.63.pair_ref, ...), custom_call_target="tpu_custom_call" | custom-call | tf_op jit(solution)/shard_map/pallas_call | solution.py:452
  104.4 5.4 %shard_map.116 = (bf16[320,1024]{1,0:T(8,128)(2,1)S(1)}, bf16[320,1024]{1,0:T(8,128)(2,1)S(1)}, bf16[320,1024]{1,0:T(8,128)(2,1)S(1)}, bf16[192,1024]{1,0:T(8,12...) custom-call(s32[4]{0:T(128)S(1)} %pad_add_fusion.here_ref, ...), custom_call_target="tpu_custom_call" | custom-call | tf_op jit(solution)/shard_map/pallas_call | solution.py:365
  118.6 8.2 %shard_map.126 = (bf16[3072,256]{1,0:T(8,128)(2,1)}, bf16[3072,256]{1,0:T(8,128)(2,1)}) custom-call(s32[4]{0:T(128)S(1)} %pad_add_fusion.here_ref, bf16[1,16,1,32,4096]{4,3,2,1,0:T(8,128)(2,1)S(1)} %copy-done, bf16[512,256]{1,0:T(8,128)(2,1)S(1)} %get-tuple-element.60.refs_12_.hidden_ref, bf16[512,512]{1,0:T(8,128)(2,1)S(1)} %get-tuple-element.63.pair_ref, ...), custom_call_target="tpu_custom_call" | custom-call | tf_op jit(solution)/shard_map/pallas_call | solution.py:452
  130.0 3.0 %shard_map.128 = bf16[3072,256]{1,0:T(8,128)(2,1)} custom-call(bf16[3072,256]{1,0:T(8,128)(2,1)} %get-tuple-element.86.whole_ref, bf16[1536,256]{1,0:T(8,128)(2,1)S(1)} %collective-permute-done.34.half_ref), custom_call_target="tpu_custom_call", output_to_operand_aliasing={{}: (0, {})} | custom-call | tf_op jit(solution)/shard_map/pallas_call | solution.py:87
  134.4 5.3 %collective-permute-start.27 = (bf16[64,1152]{1,0:T(8,128)(2,1)S(1)}, bf16[64,1152]{1,0:T(8,128)(2,1)S(1)}, u32[]{:S(2)}, u32[]{:S(2)}) collective-permute-start(bf16[64,1152]{1,0:T(8,128)(2,1)S(1)} %get-tuple-element.78), channel_id=1, source_target_pairs={{0,160},{16,176},{32,192},{48,208},{64,224},{80,240},{96,0},{112,1... | collective-permute-start | bytes 442376 | tf_op jit(solution)/shard_map/ppermute | solution.py:27
  140.0 3.3 %collective-permute-done.27.refs_5_ = bf16[64,1152]{1,0:T(8,128)(2,1)S(1)} collective-permute-done((bf16[64,1152]{1,0:T(8,128)(2,1)S(1)}, bf16[64,1152]{1,0:T(8,128)(2,1)S(1)}, u32[]{:S(2)}, u32[]{:S(2)}) %collective-permute-start.27) | collective-permute-done | bytes 147488 | tf_op jit(solution)/shard_map/ppermute | solution.py:27
  143.3 3.7 %collective-permute-done.28.refs_6_ = bf16[64,1152]{1,0:T(8,128)(2,1)S(1)} collective-permute-done((bf16[64,1152]{1,0:T(8,128)(2,1)S(1)}, bf16[64,1152]{1,0:T(8,128)(2,1)S(1)}, u32[]{:S(2)}, u32[]{:S(2)}) %collective-permute-start.28) | collective-permute-done | bytes 147488 | tf_op jit(solution)/shard_map/ppermute | solution.py:27
  147.0 5.3 %collective-permute-done.29.refs_7_ = bf16[64,1152]{1,0:T(8,128)(2,1)S(1)} collective-permute-done((bf16[64,1152]{1,0:T(8,128)(2,1)S(1)}, bf16[64,1152]{1,0:T(8,128)(2,1)S(1)}, u32[]{:S(2)}, u32[]{:S(2)}) %collective-permute-start.29) | collective-permute-done | bytes 147488 | tf_op jit(solution)/shard_map/ppermute | solution.py:27
  162.0 9.1 %collective-permute-start.30 = (bf16[256,1152]{1,0:T(8,128)(2,1)S(1)}, bf16[256,1152]{1,0:T(8,128)(2,1)S(1)}, u32[]{:S(2)}, u32[]{:S(2)}) collective-permute-start(bf16[256,1152]{1,0:T(8,128)(2,1)S(1)} %get-tuple-element.82), channel_id=1, source_target_pairs={{0,16},{16,0},{32,48},{48,32},{64,80},{80,64},{96,112},{112,96},{1... | collective-permute-start | bytes 1769480 | tf_op jit(solution)/shard_map/ppermute | solution.py:31
  176.9 5.9 %collective-permute-done.33.refs_3_ = bf16[128,1152]{1,0:T(8,128)(2,1)S(1)} collective-permute-done((bf16[128,1152]{1,0:T(8,128)(2,1)S(1)}, bf16[128,1152]{1,0:T(8,128)(2,1)S(1)}, u32[]{:S(2)}, u32[]{:S(2)}) %collective-permute-start.33) | collective-permute-done | bytes 294944 | tf_op jit(solution)/shard_map/ppermute | solution.py:22
  182.8 6.9 %collective-permute-done.32.refs_2_ = bf16[128,1152]{1,0:T(8,128)(2,1)S(1)} collective-permute-done((bf16[128,1152]{1,0:T(8,128)(2,1)S(1)}, bf16[128,1152]{1,0:T(8,128)(2,1)S(1)}, u32[]{:S(2)}, u32[]{:S(2)}) %collective-permute-start.32) | collective-permute-done | bytes 294944 | tf_op jit(solution)/shard_map/ppermute | solution.py:22
  196.7 6.4 %shard_map.130 = (f32[1024,256]{1,0:T(8,128)}, f32[1024,256]{1,0:T(8,128)}, f32[256,1024]{1,0:T(8,128)}) custom-call(s32[4]{0:T(128)S(1)} %pad_add_fusion.here_ref, bf16[1,16,1,32,4096]{4,3,2,1,0:T(8,128)(2,1)S(1)} %copy-done.1, bf16[512,256]{1,0:T(8,128)(2,1)S(1)} %get-tuple-element.60.refs_12_.hidden_ref, bf16[512,512]{1,0:T(8,128)(2,1)S(1)} %copy-done.5, ...), custom_call_target="tpu_custom_call" | custom-call | tf_op jit(solution)/shard_map/pallas_call | solution.py:452
  (111 shorter events, 63.8 us)
Async XLA Ops:
  2.3 35.3 %collective-permute-start.14 = (bf16[3072,256]{1,0:T(8,128)(2,1)S(1)}, bf16[3072,256]{1,0:T(8,128)(2,1)S(1)}, u32[]{:S(2)}, u32[]{:S(2)}) collective-permute-start(bf16[3072,256]{1,0:T(8,128)(2,1)S(1)} %shard_map.113.refs_0_.refs_7_), channel_id=1, source_target_pairs={{0,4},{4,8},{8,12},{12,0},{1,5},{5,9},{9,13},{13,1},{2,6},{6,10},{... | collective-permute-start | bytes 4718600 | tf_op jit(solution)/shard_map/ppermute | solution.py:22
  4.4 41.7 %collective-permute-start.13 = (bf16[3072,256]{1,0:T(8,128)(2,1)S(1)}, bf16[3072,256]{1,0:T(8,128)(2,1)}, u32[]{:S(2)}, u32[]{:S(2)}) collective-permute-start(bf16[3072,256]{1,0:T(8,128)(2,1)S(1)} %shard_map.113.refs_0_.refs_7_), channel_id=1, source_target_pairs={{0,12},{4,0},{8,4},{12,8},{1,13},{5,1},{9,5},{13,9},{2,14},{6,2},{... | collective-permute-start | bytes 4718600 | tf_op jit(solution)/shard_map/ppermute | solution.py:22
  29.4 32.1 %collective-permute-start.6 = (bf16[320,1024]{1,0:T(8,128)(2,1)S(1)}, bf16[320,1024]{1,0:T(8,128)(2,1)S(1)}, u32[]{:S(2)}, u32[]{:S(2)}) collective-permute-start(bf16[320,1024]{1,0:T(8,128)(2,1)S(1)} %shard_map.111.refs_0_), channel_id=1, source_target_pairs={{0,1},{1,2},{2,3},{3,0},{4,5},{5,6},{6,7},{7,4},{8,9},{9,10},{10,1... | collective-permute-start | bytes 1966088 | tf_op jit(solution)/shard_map/ppermute | solution.py:22
  30.8 30.8 %collective-permute-start.5 = (bf16[320,1024]{1,0:T(8,128)(2,1)S(1)}, bf16[320,1024]{1,0:T(8,128)(2,1)S(1)}, u32[]{:S(2)}, u32[]{:S(2)}) collective-permute-start(bf16[320,1024]{1,0:T(8,128)(2,1)S(1)} %shard_map.111.refs_0_), channel_id=1, source_target_pairs={{0,3},{1,0},{2,1},{3,2},{4,7},{5,4},{6,5},{7,6},{8,11},{9,8},{10,9... | collective-permute-start | bytes 1966088 | tf_op jit(solution)/shard_map/ppermute | solution.py:22
  32.3 15.7 %collective-permute-start.7 = (bf16[64,1024]{1,0:T(8,128)(2,1)S(1)}, bf16[64,1024]{1,0:T(8,128)(2,1)S(1)}, u32[]{:S(2)}, u32[]{:S(2)}) collective-permute-start(bf16[64,1024]{1,0:T(8,128)(2,1)S(1)} %get-tuple-element.54), channel_id=1, source_target_pairs={{0,96},{16,112},{32,128},{48,144},{64,160},{80,176},{96,192},{112,... | collective-permute-start | bytes 393224 | tf_op jit(solution)/shard_map/ppermute | solution.py:27
  37.6 22.4 %collective-permute-start.8 = (bf16[64,1024]{1,0:T(8,128)(2,1)S(1)}, bf16[64,1024]{1,0:T(8,128)(2,1)S(1)}, u32[]{:S(2)}, u32[]{:S(2)}) collective-permute-start(bf16[64,1024]{1,0:T(8,128)(2,1)S(1)} %get-tuple-element.55), channel_id=1, source_target_pairs={{0,160},{16,176},{32,192},{48,208},{64,224},{80,240},{96,0},{112,1... | collective-permute-start | bytes 393224 | tf_op jit(solution)/shard_map/ppermute | solution.py:27
  46.1 15.4 %collective-permute-start.9 = (bf16[64,1024]{1,0:T(8,128)(2,1)S(1)}, bf16[64,1024]{1,0:T(8,128)(2,1)S(1)}, u32[]{:S(2)}, u32[]{:S(2)}) collective-permute-start(bf16[64,1024]{1,0:T(8,128)(2,1)S(1)} %get-tuple-element.56), channel_id=1, source_target_pairs={{0,128},{16,144},{32,160},{48,176},{64,192},{80,208},{96,224},{112... | collective-permute-start | bytes 393224 | tf_op jit(solution)/shard_map/ppermute | solution.py:27
  48.0 18.5 %collective-permute-start.15 = (bf16[1536,256]{1,0:T(8,128)(2,1)S(1)}, bf16[1536,256]{1,0:T(8,128)(2,1)S(1)}, u32[]{:S(2)}, u32[]{:S(2)}) collective-permute-start(bf16[1536,256]{1,0:T(8,128)(2,1)S(1)} %slice.18), channel_id=1, source_target_pairs={{0,4},{4,8},{8,12},{12,0},{1,5},{5,9},{9,13},{13,1},{2,6},{6,10},{... | collective-permute-start | bytes 2359304 | tf_op jit(solution)/shard_map/ppermute | solution.py:22
  60.0 18.0 %collective-permute-start.16 = (bf16[1536,256]{1,0:T(8,128)(2,1)S(1)}, bf16[1536,256]{1,0:T(8,128)(2,1)S(1)}, u32[]{:S(2)}, u32[]{:S(2)}) collective-permute-start(bf16[1536,256]{1,0:T(8,128)(2,1)S(1)} %slice.19), channel_id=1, source_target_pairs={{0,12},{4,0},{8,4},{12,8},{1,13},{5,1},{9,5},{13,9},{2,14},{6,2},{... | collective-permute-start | bytes 2359304 | tf_op jit(solution)/shard_map/ppermute | solution.py:22
  61.6 27.8 %collective-permute-start.10 = (bf16[352,1024]{1,0:T(8,128)(2,1)S(1)}, bf16[352,1024]{1,0:T(8,128)(2,1)S(1)}, u32[]{:S(2)}, u32[]{:S(2)}) collective-permute-start(bf16[352,1024]{1,0:T(8,128)(2,1)S(1)} %get-tuple-element.58), channel_id=1, source_target_pairs={{0,3},{1,0},{2,1},{3,2},{4,7},{5,4},{6,5},{7,6},{8,11},{9,8},{10,9... | collective-permute-start | bytes 2162696 | tf_op jit(solution)/shard_map/ppermute | solution.py:22
  64.6 24.8 %collective-permute-start.11 = (bf16[352,1024]{1,0:T(8,128)(2,1)S(1)}, bf16[352,1024]{1,0:T(8,128)(2,1)S(1)}, u32[]{:S(2)}, u32[]{:S(2)}) collective-permute-start(bf16[352,1024]{1,0:T(8,128)(2,1)S(1)} %get-tuple-element.59), channel_id=1, source_target_pairs={{0,1},{1,2},{2,3},{3,0},{4,5},{5,6},{6,7},{7,4},{8,9},{9,10},{10,1... | collective-permute-start | bytes 2162696 | tf_op jit(solution)/shard_map/ppermute | solution.py:22
  64.6 24.8 %collective-permute-start.12 = (bf16[192,1024]{1,0:T(8,128)(2,1)S(1)}, bf16[192,1024]{1,0:T(8,128)(2,1)S(1)}, u32[]{:S(2)}, u32[]{:S(2)}) collective-permute-start(bf16[192,1024]{1,0:T(8,128)(2,1)S(1)} %get-tuple-element.57.refs_3_), channel_id=1, source_target_pairs={{0,2},{1,3},{2,0},{3,1},{4,6},{5,7},{6,4},{7,5},{8,10},{9,11},{10,... | collective-permute-start | bytes 1179656 | tf_op jit(solution)/shard_map/ppermute | solution.py:22
  100.2 15.8 %collective-permute-start.36 = (bf16[1536,256]{1,0:T(8,128)(2,1)S(1)}, bf16[1536,256]{1,0:T(8,128)(2,1)S(1)}, u32[]{:S(2)}, u32[]{:S(2)}) collective-permute-start(bf16[1536,256]{1,0:T(8,128)(2,1)S(1)} %get-tuple-element.89), channel_id=1, source_target_pairs={{0,12},{4,0},{8,4},{12,8},{1,13},{5,1},{9,5},{13,9},{2,14},{6,2},{... | collective-permute-start | bytes 2359304 | tf_op jit(solution)/shard_map/ppermute | solution.py:22
  103.5 26.3 %collective-permute-start.34 = (bf16[1536,256]{1,0:T(8,128)(2,1)S(1)}, bf16[1536,256]{1,0:T(8,128)(2,1)S(1)}, u32[]{:S(2)}, u32[]{:S(2)}) collective-permute-start(bf16[1536,256]{1,0:T(8,128)(2,1)S(1)} %get-tuple-element.87), channel_id=1, source_target_pairs={{0,4},{4,8},{8,12},{12,0},{1,5},{5,9},{9,13},{13,1},{2,6},{6,10},{... | collective-permute-start | bytes 2359304 | tf_op jit(solution)/shard_map/ppermute | solution.py:22
  112.1 20.9 %collective-permute-start.25 = (bf16[192,1024]{1,0:T(8,128)(2,1)S(1)}, bf16[192,1024]{1,0:T(8,128)(2,1)S(1)}, u32[]{:S(2)}, u32[]{:S(2)}) collective-permute-start(bf16[192,1024]{1,0:T(8,128)(2,1)S(1)} %shard_map.120), channel_id=1, source_target_pairs={{0,1},{1,2},{2,3},{3,0},{4,5},{5,6},{6,7},{7,4},{8,9},{9,10},{10,1... | collective-permute-start | bytes 1179656 | tf_op jit(solution)/shard_map/ppermute | solution.py:22
  112.4 27.2 %collective-permute-start.20 = (bf16[320,1024]{1,0:T(8,128)(2,1)S(1)}, bf16[320,1024]{1,0:T(8,128)(2,1)S(1)}, u32[]{:S(2)}, u32[]{:S(2)}) collective-permute-start(bf16[320,1024]{1,0:T(8,128)(2,1)S(1)} %shard_map.118), channel_id=1, source_target_pairs={{0,3},{1,0},{2,1},{3,2},{4,7},{5,4},{6,5},{7,6},{8,11},{9,8},{10,9... | collective-permute-start | bytes 1966088 | tf_op jit(solution)/shard_map/ppermute | solution.py:22
  115.4 24.2 %collective-permute-start.18 = (bf16[320,1024]{1,0:T(8,128)(2,1)S(1)}, bf16[320,1024]{1,0:T(8,128)(2,1)S(1)}, u32[]{:S(2)}, u32[]{:S(2)}) collective-permute-start(bf16[320,1024]{1,0:T(8,128)(2,1)S(1)} %shard_map.117), channel_id=1, source_target_pairs={{0,1},{1,2},{2,3},{3,0},{4,5},{5,6},{6,7},{7,4},{8,9},{9,10},{10,1... | collective-permute-start | bytes 1966088 | tf_op jit(solution)/shard_map/ppermute | solution.py:22
  116.1 18.2 %collective-permute-start.26 = (bf16[192,1024]{1,0:T(8,128)(2,1)S(1)}, bf16[192,1024]{1,0:T(8,128)(2,1)S(1)}, u32[]{:S(2)}, u32[]{:S(2)}) collective-permute-start(bf16[192,1024]{1,0:T(8,128)(2,1)S(1)} %shard_map.121), channel_id=1, source_target_pairs={{0,3},{1,0},{2,1},{3,2},{4,7},{5,4},{6,5},{7,6},{8,11},{9,8},{10,9... | collective-permute-start | bytes 1179656 | tf_op jit(solution)/shard_map/ppermute | solution.py:22
  129.8 62.5 %collective-permute-start.37 = (bf16[3072,256]{1,0:T(8,128)(2,1)}, bf16[3072,256]{1,0:T(8,128)(2,1)S(1)}, u32[]{:S(2)}, u32[]{:S(2)}) collective-permute-start(bf16[3072,256]{1,0:T(8,128)(2,1)} %shard_map.129), channel_id=1, source_target_pairs={{0,12},{4,0},{8,4},{12,8},{1,13},{5,1},{9,5},{13,9},{2,14},{6,2},{... | collective-permute-start | bytes 4718600 | tf_op jit(solution)/shard_map/ppermute | solution.py:22
  133.0 59.3 %collective-permute-start.35 = (bf16[3072,256]{1,0:T(8,128)(2,1)}, bf16[3072,256]{1,0:T(8,128)(2,1)}, u32[]{:S(2)}, u32[]{:S(2)}) collective-permute-start(bf16[3072,256]{1,0:T(8,128)(2,1)} %shard_map.128), channel_id=1, source_target_pairs={{0,4},{4,8},{8,12},{12,0},{1,5},{5,9},{9,13},{13,1},{2,6},{6,10},{... | collective-permute-start | bytes 4718600 | tf_op jit(solution)/shard_map/ppermute | solution.py:22
  139.6 12.6 %collective-permute-start.29 = (bf16[64,1152]{1,0:T(8,128)(2,1)S(1)}, bf16[64,1152]{1,0:T(8,128)(2,1)S(1)}, u32[]{:S(2)}, u32[]{:S(2)}) collective-permute-start(bf16[64,1152]{1,0:T(8,128)(2,1)S(1)} %get-tuple-element.80), channel_id=1, source_target_pairs={{0,128},{16,144},{32,160},{48,176},{64,192},{80,208},{96,224},{112... | collective-permute-start | bytes 442376 | tf_op jit(solution)/shard_map/ppermute | solution.py:27
  147.0 11.9 %collective-permute-start.22 = (bf16[64,1152]{1,0:T(8,128)(2,1)S(1)}, bf16[64,1152]{1,0:T(8,128)(2,1)S(1)}, u32[]{:S(2)}, u32[]{:S(2)}) collective-permute-start(bf16[64,1152]{1,0:T(8,128)(2,1)S(1)} %get-tuple-element.72), channel_id=1, source_target_pairs={{0,32},{16,48},{32,64},{48,80},{64,96},{80,112},{96,128},{112,144}... | collective-permute-start | bytes 442376 | tf_op jit(solution)/shard_map/ppermute | solution.py:27
  174.1 15.7 %collective-permute-start.32 = (bf16[128,1152]{1,0:T(8,128)(2,1)S(1)}, bf16[128,1152]{1,0:T(8,128)(2,1)S(1)}, u32[]{:S(2)}, u32[]{:S(2)}) collective-permute-start(bf16[128,1152]{1,0:T(8,128)(2,1)S(1)} %shard_map.124.refs_0_), channel_id=1, source_target_pairs={{0,2},{1,3},{2,0},{3,1},{4,6},{5,7},{6,4},{7,5},{8,10},{9,11},{10,... | collective-permute-start | bytes 884744 | tf_op jit(solution)/shard_map/ppermute | solution.py:22
  176.7 13.0 %collective-permute-start.31 = (bf16[128,1152]{1,0:T(8,128)(2,1)S(1)}, bf16[128,1152]{1,0:T(8,128)(2,1)S(1)}, u32[]{:S(2)}, u32[]{:S(2)}) collective-permute-start(bf16[128,1152]{1,0:T(8,128)(2,1)S(1)} %shard_map.124.refs_0_), channel_id=1, source_target_pairs={{0,3},{1,0},{2,1},{3,2},{4,7},{5,4},{6,5},{7,6},{8,11},{9,8},{10,9... | collective-permute-start | bytes 884744 | tf_op jit(solution)/shard_map/ppermute | solution.py:22
  (22 other events, 243.1 us)
where the time goes:
time: 204 us; the launch traced here: 203 us
  waiting for transfers between devices  76 us (37%)
  starting transfers between devices  65 us (32%)
  Pallas kernels  49.1 us (24%)
  local copies, waits for them, and re-layouts  6.9 us (3%)
  matrix products  3 us (1%)
  other arithmetic  2.09 us (1%)
    ppermute x14, waiting for transfers between devices, shift_z(): return lax.ppermute(x, 'ep', [(i, (i + 2 * step) % n) for i in range(n)])  37.4 us
    ppermute x22, waiting for transfers between devices, shift(): return lax.ppermute(x, axis, [(i, (i + step) % n) for i in range(n)])  36.9 us
    ppermute x22, starting transfers between devices, shift(): return lax.ppermute(x, axis, [(i, (i + step) % n) for i in range(n)])  28.3 us
    ppermute x14, starting transfers between devices, shift_z(): return lax.ppermute(x, 'ep', [(i, (i + 2 * step) % n) for i in range(n)])  24.5 us
    pallas_call x3, Pallas kernels, weight_chunk(): call(kernel, outs, mib=18 if received else 14, grid_spec=pltpu.PrefetchSc...  18.1 us
    ppermute x2, starting transfers between devices, swap_cores(): lax.ppermute(x, 'ep', [(i, i ^ 1) for i in range(lax.axis_size('ep'))])  12.2 us
    pallas_call x1, Pallas kernels, pair_gradients(): call(kernel, tuple(outs), mib=24, grid_spec=pltpu.PrefetchScalarGridSpec(...  7.21 us
    pallas_call x1, Pallas kernels, activations(): call(kernel, (bf16(slots, width), f32(slots, width), f32(slots, width)),...  6.86 us
  transfers between devices with their start and end apart: 38, of which 20 were waited for; matrix products, arithmetic and copies ran while one was open for 4% of the time, Pallas kernels for 15%

commit v1 on v0

--- a/solution.py
+++ b/solution.py
@@ -218,7 +218,40 @@
     )(here, routed_inputs, *weights)
 
 
-def pair_gradients(here, arrays, places, weights, hidden, silu, slope, groups):
+def pick_weights(here, weights):
+    width = weights[0].shape[1]
+    depth = weights[0].shape[0] // 3
+
+    def kernel(here_ref, *refs):
+        weight_refs, (downs, chosen, sem, sems) = refs[:5], refs[5:]
+        start_select(weight_refs, (here_ref[1] + 2) % RING, chosen, sem, depth)
+        copies = []
+        for r in range(RING):
+            ((ref, first, count),) = weight_parts(weight_refs, r, depth)[2]
+            source = ref.at[pl.ds(first, count)]
+            copies.append(pltpu.make_async_copy(source, downs.at[r], sems.at[r]))
+        for copy in copies:
+            copy.start()
+        for copy in copies:
+            copy.wait()
+        wait_select(chosen, sem)
+
+    whole = pl.BlockSpec(memory_space=pltpu.VMEM)
+    return call(
+        kernel,
+        (bf16(RING, depth, width), bf16(2 * depth, width)),
+        mib=12,
+        grid_spec=pltpu.PrefetchScalarGridSpec(
+            num_scalar_prefetch=1,
+            grid=(1,),
+            in_specs=[whole] * 5,
+            out_specs=(whole,) * 2,
+            scratch_shapes=[pltpu.SemaphoreType.DMA, pltpu.SemaphoreType.DMA((RING,))],
+        ),
+    )(here, *weights)
+
+
+def pair_gradients(here, arrays, places, picked, hidden, silu, slope, groups):
     slots, width = hidden.shape
     depth = arrays[0].shape[1]
     spans, at = [], 0
@@ -228,23 +261,17 @@
 
     def kernel(here_ref, *refs):
         scaled_refs, refs = refs[: len(arrays)], refs[len(arrays) :]
-        weight_refs, (hidden_ref, silu_ref, slope_ref) = refs[:5], refs[5:8]
-        pair_ref, extra_ref, by_r, top_ref, bottom_ref = refs[8:13]
-        chosen, downs, hidden_grad_ref, chosen_sem, sems = refs[13:]
+        downs, chosen, hidden_ref, silu_ref, slope_ref = refs[:5]
+        pair_ref, extra_ref, by_r, top_ref, bottom_ref, hidden_grad_ref, sems = refs[5:]
         t = here_ref[1]
         for array, first, q, slot, count in places:
             r = (t + q) % RING
             source = scaled_refs[array].at[pl.ds(first, count)]
-            pltpu.make_async_copy(source, by_r.at[r, pl.ds(slot, count)], sems.at[0, r]).start()
-        for r in range(RING):
-            ((ref, first, count),) = weight_parts(weight_refs, r, depth)[2]
-            pltpu.make_async_copy(ref.at[pl.ds(first, count)], downs.at[r], sems.at[1, r]).start()
-        start_select(weight_refs, (t + 2) % RING, chosen, chosen_sem, depth)
+            pltpu.make_async_copy(source, by_r.at[r, pl.ds(slot, count)], sems.at[r]).start()
         hidden_grad_ref[...] = jnp.zeros_like(hidden_grad_ref)
 
         def add_columns(r, carry):
-            pltpu.make_async_copy(by_r.at[r], by_r.at[r], sems.at[0, r]).wait()
-            pltpu.make_async_copy(downs.at[r], downs.at[r], sems.at[1, r]).wait()
+            pltpu.make_async_copy(by_r.at[r], by_r.at[r], sems.at[r]).wait()
             hidden_grad_ref[...] += dot(by_r[r], downs[r])
             return carry
 
@@ -265,7 +292,6 @@
             return carry
 
         lax.fori_loop(0, slots // LANES, finish, 0)
-        wait_select(chosen, chosen_sem)
 
         def put(columns, value):
             for start, rows in spans:
@@ -287,17 +313,14 @@
         grid_spec=pltpu.PrefetchScalarGridSpec(
             num_scalar_prefetch=1,
             grid=(1,),
-            in_specs=[anywhere] * len(arrays) + [whole] * 8,
+            in_specs=[anywhere] * len(arrays) + [whole] * 5,
             out_specs=(whole,) * len(outs),
             scratch_shapes=[
-                pltpu.VMEM((2 * depth, width), jnp.bfloat16),
-                pltpu.VMEM((RING, depth, width), jnp.bfloat16),
                 pltpu.VMEM((slots, width), jnp.float32),
-                pltpu.SemaphoreType.DMA,
-                pltpu.SemaphoreType.DMA((2, RING)),
+                pltpu.SemaphoreType.DMA((RING,)),
             ],
         ),
-    )(here, *arrays, *weights, hidden, silu, slope)
+    )(here, *arrays, *picked, hidden, silu, slope)
 
 
 def slot_part(pair_ref, weights, depth, put):
@@ -660,7 +683,7 @@
 
     hidden, silu, slope = activations(here, routed_inputs, weights, width)
     pair, extra, scaled, *far = pair_gradients(
-        here, arrays, places, weights, hidden, silu, slope, groups
+        here, arrays, places, pick_weights(here, weights), hidden, silu, slope, groups
     )
     far = far_halves(*far, "tp")
     parts = slot_gradients(here, pair, weights, groups)

time: 204 us -> 204 us (level)
    ppermute x14, waiting for transfers between devices: 37.4 us -> 40.8 us  [shift_z(): return lax.ppermute(x, 'ep', [(i, (i + 2 * step) % n) for i in range(n)])]
    ppermute x22, starting transfers between devices: 28.3 us -> 31.6 us  [shift(): return lax.ppermute(x, axis, [(i, (i + step) % n) for i in range(n)])]
    ppermute x14, starting transfers between devices: 24.5 us -> 21.4 us  [shift_z(): return lax.ppermute(x, 'ep', [(i, (i + 2 * step) % n) for i in range(n)])]
    ppermute x22, waiting for transfers between devices: 36.9 us -> 34.1 us  [shift(): return lax.ppermute(x, axis, [(i, (i + step) % n) for i in range(n)])]
    pallas_call x0 -> x1, Pallas kernels: none -> 2.48 us  [pick_weights(): call(kernel, (bf16(RING, depth, width), bf16(2 * depth, width)), mib=12,...]
  transfers between devices with their start and end apart: 38 -> 38, of which waited for: 20 -> 19; matrix products, arithmetic and copies ran while one was open for 4% -> 4% of each run, Pallas kernels for 15% -> 16%
where the time goes in v1:
time: 204 us
  waiting for transfers between devices  76.6 us (38%)
  starting transfers between devices  64.4 us (32%)
  Pallas kernels  49.7 us (24%)
  local copies, waits for them, and re-layouts  6.92 us (3%)
  matrix products  3 us (1%)
  other arithmetic  2.09 us (1%)
    ppermute x14, waiting for transfers between devices, shift_z(): return lax.ppermute(x, 'ep', [(i, (i + 2 * step) % n) for i in range(n)])  40.8 us
    ppermute x22, waiting for transfers between devices, shift(): return lax.ppermute(x, axis, [(i, (i + step) % n) for i in range(n)])  34.1 us
    ppermute x22, starting transfers between devices, shift(): return lax.ppermute(x, axis, [(i, (i + step) % n) for i in range(n)])  31.6 us
    ppermute x14, starting transfers between devices, shift_z(): return lax.ppermute(x, 'ep', [(i, (i + 2 * step) % n) for i in range(n)])  21.4 us
    pallas_call x3, Pallas kernels, weight_chunk(): call(kernel, outs, mib=18 if received else 14, grid_spec=pltpu.PrefetchSc...  18.1 us
    ppermute x2, starting transfers between devices, swap_cores(): lax.ppermute(x, 'ep', [(i, i ^ 1) for i in range(lax.axis_size('ep'))])  11.4 us
    pallas_call x1, Pallas kernels, activations(): call(kernel, (bf16(slots, width), f32(slots, width), f32(slots, width)),...  6.85 us
    pallas_call x6, Pallas kernels, add_half(): call(kernel, bf16(*whole.shape), grid=(blocks,), in_specs=[spec, pl.Block...  6.66 us
  transfers between devices with their start and end apart: 38, of which 19 were waited for; matrix products, arithmetic and copies ran while one was open for 4% of the time, Pallas kernels for 16%

profile of v1, /device:TPU:1, one launch (start us, length us, event | category | flops | bytes accessed | tf_op | source)
XLA Modules:
  0.0 203.7 jit_solution(8508733830850383178)
XLA Ops:
  9.9 3.1 %collective-permute-start = (bf16[256,1024]{1,0:T(8,128)(2,1)S(1)}, bf16[256,1024]{1,0:T(8,128)(2,1)S(1)}, u32[]{:S(2)}, u32[]{:S(2)}) collective-permute-start(bf16[256,1024]{1,0:T(8,128)(2,1)S(1)} %fusion.1), channel_id=1, source_target_pairs={{0,16},{16,0},{32,48},{48,32},{64,80},{80,64},{96,112},{112,96},{1... | collective-permute-start | bytes 1572872 | tf_op jit(solution)/shard_map/ppermute | solution.py:31
  14.7 3.9 %collective-permute-start.2 = (bf16[64,1024]{1,0:T(8,128)(2,1)S(1)}, bf16[64,1024]{1,0:T(8,128)(2,1)S(1)}, u32[]{:S(2)}, u32[]{:S(2)}) collective-permute-start(bf16[64,1024]{1,0:T(8,128)(2,1)S(1)} %get-tuple-element.53), channel_id=1, source_target_pairs={{0,224},{16,240},{32,0},{48,16},{64,32},{80,48},{96,64},{112,80},{... | collective-permute-start | bytes 393224 | tf_op jit(solution)/shard_map/ppermute | solution.py:27
  18.7 3.4 %collective-permute-done.1.refs_1_ = bf16[64,1024]{1,0:T(8,128)(2,1)S(1)} collective-permute-done((bf16[64,1024]{1,0:T(8,128)(2,1)S(1)}, bf16[64,1024]{1,0:T(8,128)(2,1)S(1)}, u32[]{:S(2)}, u32[]{:S(2)}) %collective-permute-start.1) | collective-permute-done | bytes 131104 | tf_op jit(solution)/shard_map/ppermute | solution.py:27
  23.8 4.0 %collective-permute-done.3.refs_3_ = bf16[64,1024]{1,0:T(8,128)(2,1)S(1)} collective-permute-done((bf16[64,1024]{1,0:T(8,128)(2,1)S(1)}, bf16[64,1024]{1,0:T(8,128)(2,1)S(1)}, u32[]{:S(2)}, u32[]{:S(2)}) %collective-permute-start.3) | collective-permute-done | bytes 131104 | tf_op jit(solution)/shard_map/ppermute | solution.py:27
  32.3 5.3 %collective-permute-done.14.refs_4_ = bf16[3072,256]{1,0:T(8,128)(2,1)S(1)} collective-permute-done((bf16[3072,256]{1,0:T(8,128)(2,1)S(1)}, bf16[3072,256]{1,0:T(8,128)(2,1)S(1)}, u32[]{:S(2)}, u32[]{:S(2)}) %collective-permute-start.14) | collective-permute-done | bytes 1572896 | tf_op jit(solution)/shard_map/ppermute | solution.py:22
  37.6 8.6 %collective-permute-start.8 = (bf16[64,1024]{1,0:T(8,128)(2,1)S(1)}, bf16[64,1024]{1,0:T(8,128)(2,1)S(1)}, u32[]{:S(2)}, u32[]{:S(2)}) collective-permute-start(bf16[64,1024]{1,0:T(8,128)(2,1)S(1)} %get-tuple-element.57), channel_id=1, source_target_pairs={{0,160},{16,176},{32,192},{48,208},{64,224},{80,240},{96,0},{112,1... | collective-permute-start | bytes 393224 | tf_op jit(solution)/shard_map/ppermute | solution.py:27
  48.9 11.0 %collective-permute-done.8.refs_1_ = bf16[64,1024]{1,0:T(8,128)(2,1)S(1)} collective-permute-done((bf16[64,1024]{1,0:T(8,128)(2,1)S(1)}, bf16[64,1024]{1,0:T(8,128)(2,1)S(1)}, u32[]{:S(2)}, u32[]{:S(2)}) %collective-permute-start.8) | collective-permute-done | bytes 131104 | tf_op jit(solution)/shard_map/ppermute | solution.py:27
  61.6 3.0 %collective-permute-start.10 = (bf16[352,1024]{1,0:T(8,128)(2,1)S(1)}, bf16[352,1024]{1,0:T(8,128)(2,1)S(1)}, u32[]{:S(2)}, u32[]{:S(2)}) collective-permute-start(bf16[352,1024]{1,0:T(8,128)(2,1)S(1)} %get-tuple-element.60), channel_id=1, source_target_pairs={{0,3},{1,0},{2,1},{3,2},{4,7},{5,4},{6,5},{7,6},{8,11},{9,8},{10,9... | collective-permute-start | bytes 2162696 | tf_op jit(solution)/shard_map/ppermute | solution.py:22
  66.4 11.6 %collective-permute-done.16.refs_3_ = bf16[1536,256]{1,0:T(8,128)(2,1)S(1)} collective-permute-done((bf16[1536,256]{1,0:T(8,128)(2,1)S(1)}, bf16[1536,256]{1,0:T(8,128)(2,1)S(1)}, u32[]{:S(2)}, u32[]{:S(2)}) %collective-permute-start.16) | collective-permute-done | bytes 786464 | tf_op jit(solution)/shard_map/ppermute | solution.py:22
  80.7 6.9 %shard_map.115 = (bf16[512,256]{1,0:T(8,128)(2,1)S(1)}, f32[512,256]{1,0:T(8,128)S(1)}, f32[512,256]{1,0:T(8,128)S(1)}) custom-call(s32[4]{0:T(128)S(1)} %pad_add_fusion.here_ref, bf16[1,16,1,32,4096]{4,3,2,1,0:T(8,128)(2,1)S(1)} %copy-done, bf16[3072,256]{1,0:T(8,128)(2,1)S(1)} %shard_map.113.refs_0_, bf16[3072,256]{1,0:T(8,128)(2,1)} %collective-permute-done.13.refs_1_, ...), custom_call_target="tpu_custom_call" | custom-call | tf_op jit(solution)/shard_map/pallas_call | solution.py:199
  89.5 5.4 %shard_map.116 = (bf16[512,512]{1,0:T(8,128)(2,1)S(1)}, bf16[512,128]{1,0:T(8,128)(2,1)S(1)}, bf16[4,512,1024]{2,1,0:T(8,128)(2,1)S(1)}, bf16[256,1024]{1,0:T(8,128)(2,1)S(1)}, bf16[256,1024]{1,0:T(8,128)(2,1)S(1)}) custom-call(s32[4]{0:T(128)S(1)} %pad_add_fusion.here_ref, bf16[320,1024]{1,0:T(8,128)(2,1)S(1)} %shard_map.111.refs_0_, ...), custom_call_target="tpu_custom_call" | custom-call | tf_op jit(solution)/shard_map/pallas_call | solution.py:309
  94.9 3.5 %shard_map.128 = (bf16[1536,256]{1,0:T(8,128)(2,1)S(1)}, bf16[1536,256]{1,0:T(8,128)(2,1)S(1)}) custom-call(s32[4]{0:T(128)S(1)} %pad_add_fusion.here_ref, bf16[1,16,1,32,4096]{4,3,2,1,0:T(8,128)(2,1)S(1)} %copy-done, bf16[512,256]{1,0:T(8,128)(2,1)S(1)} %get-tuple-element.64.refs_9_.hidden_ref, bf16[512,512]{1,0:T(8,128)(2,1)S(1)} %get-tuple-element.67.pair_ref, ...), custom_call_target="tpu_custom_call" | custom-call | tf_op jit(solution)/shard_map/pallas_call | solution.py:475
  102.7 5.4 %shard_map.117 = (bf16[320,1024]{1,0:T(8,128)(2,1)S(1)}, bf16[320,1024]{1,0:T(8,128)(2,1)S(1)}, bf16[320,1024]{1,0:T(8,128)(2,1)S(1)}, bf16[192,1024]{1,0:T(8,12...) custom-call(s32[4]{0:T(128)S(1)} %pad_add_fusion.here_ref, ...), custom_call_target="tpu_custom_call" | custom-call | tf_op jit(solution)/shard_map/pallas_call | solution.py:388
  114.8 3.0 %collective-permute-start.26 = (bf16[192,1024]{1,0:T(8,128)(2,1)S(1)}, bf16[192,1024]{1,0:T(8,128)(2,1)S(1)}, u32[]{:S(2)}, u32[]{:S(2)}) collective-permute-start(bf16[192,1024]{1,0:T(8,128)(2,1)S(1)} %shard_map.122), channel_id=1, source_target_pairs={{0,3},{1,0},{2,1},{3,2},{4,7},{5,4},{6,5},{7,6},{8,11},{9,8},{10,9... | collective-permute-start | bytes 1179656 | tf_op jit(solution)/shard_map/ppermute | solution.py:22
  117.7 8.2 %shard_map.127 = (bf16[3072,256]{1,0:T(8,128)(2,1)}, bf16[3072,256]{1,0:T(8,128)(2,1)}) custom-call(s32[4]{0:T(128)S(1)} %pad_add_fusion.here_ref, bf16[1,16,1,32,4096]{4,3,2,1,0:T(8,128)(2,1)S(1)} %copy-done, bf16[512,256]{1,0:T(8,128)(2,1)S(1)} %get-tuple-element.64.refs_9_.hidden_ref, bf16[512,512]{1,0:T(8,128)(2,1)S(1)} %get-tuple-element.67.pair_ref, ...), custom_call_target="tpu_custom_call" | custom-call | tf_op jit(solution)/shard_map/pallas_call | solution.py:475
  131.8 2.9 %shard_map.129 = bf16[3072,256]{1,0:T(8,128)(2,1)} custom-call(bf16[3072,256]{1,0:T(8,128)(2,1)} %get-tuple-element.90.whole_ref, bf16[1536,256]{1,0:T(8,128)(2,1)S(1)} %collective-permute-done.34.half_ref), custom_call_target="tpu_custom_call", output_to_operand_aliasing={{}: (0, {})} | custom-call | tf_op jit(solution)/shard_map/pallas_call | solution.py:87
  134.9 5.3 %collective-permute-start.27 = (bf16[64,1152]{1,0:T(8,128)(2,1)S(1)}, bf16[64,1152]{1,0:T(8,128)(2,1)S(1)}, u32[]{:S(2)}, u32[]{:S(2)}) collective-permute-start(bf16[64,1152]{1,0:T(8,128)(2,1)S(1)} %get-tuple-element.82), channel_id=1, source_target_pairs={{0,160},{16,176},{32,192},{48,208},{64,224},{80,240},{96,0},{112,1... | collective-permute-start | bytes 442376 | tf_op jit(solution)/shard_map/ppermute | solution.py:27
  140.6 4.4 %collective-permute-done.27.refs_5_ = bf16[64,1152]{1,0:T(8,128)(2,1)S(1)} collective-permute-done((bf16[64,1152]{1,0:T(8,128)(2,1)S(1)}, bf16[64,1152]{1,0:T(8,128)(2,1)S(1)}, u32[]{:S(2)}, u32[]{:S(2)}) %collective-permute-start.27) | collective-permute-done | bytes 147488 | tf_op jit(solution)/shard_map/ppermute | solution.py:27
  145.0 4.1 %collective-permute-done.28.refs_6_ = bf16[64,1152]{1,0:T(8,128)(2,1)S(1)} collective-permute-done((bf16[64,1152]{1,0:T(8,128)(2,1)S(1)}, bf16[64,1152]{1,0:T(8,128)(2,1)S(1)}, u32[]{:S(2)}, u32[]{:S(2)}) %collective-permute-start.28) | collective-permute-done | bytes 147488 | tf_op jit(solution)/shard_map/ppermute | solution.py:27
  149.1 5.2 %collective-permute-done.29.refs_7_ = bf16[64,1152]{1,0:T(8,128)(2,1)S(1)} collective-permute-done((bf16[64,1152]{1,0:T(8,128)(2,1)S(1)}, bf16[64,1152]{1,0:T(8,128)(2,1)S(1)}, u32[]{:S(2)}, u32[]{:S(2)}) %collective-permute-start.29) | collective-permute-done | bytes 147488 | tf_op jit(solution)/shard_map/ppermute | solution.py:27
  162.8 8.2 %collective-permute-start.30 = (bf16[256,1152]{1,0:T(8,128)(2,1)S(1)}, bf16[256,1152]{1,0:T(8,128)(2,1)S(1)}, u32[]{:S(2)}, u32[]{:S(2)}) collective-permute-start(bf16[256,1152]{1,0:T(8,128)(2,1)S(1)} %get-tuple-element.86), channel_id=1, source_target_pairs={{0,16},{16,0},{32,48},{48,32},{64,80},{80,64},{96,112},{112,96},{1... | collective-permute-start | bytes 1769480 | tf_op jit(solution)/shard_map/ppermute | solution.py:31
  178.2 4.9 %collective-permute-done.33.refs_3_ = bf16[128,1152]{1,0:T(8,128)(2,1)S(1)} collective-permute-done((bf16[128,1152]{1,0:T(8,128)(2,1)S(1)}, bf16[128,1152]{1,0:T(8,128)(2,1)S(1)}, u32[]{:S(2)}, u32[]{:S(2)}) %collective-permute-start.33) | collective-permute-done | bytes 294944 | tf_op jit(solution)/shard_map/ppermute | solution.py:22
  183.1 7.3 %collective-permute-done.32.refs_2_ = bf16[128,1152]{1,0:T(8,128)(2,1)S(1)} collective-permute-done((bf16[128,1152]{1,0:T(8,128)(2,1)S(1)}, bf16[128,1152]{1,0:T(8,128)(2,1)S(1)}, u32[]{:S(2)}, u32[]{:S(2)}) %collective-permute-start.32) | collective-permute-done | bytes 294944 | tf_op jit(solution)/shard_map/ppermute | solution.py:22
  197.3 6.4 %shard_map.131 = (f32[1024,256]{1,0:T(8,128)}, f32[1024,256]{1,0:T(8,128)}, f32[256,1024]{1,0:T(8,128)}) custom-call(s32[4]{0:T(128)S(1)} %pad_add_fusion.here_ref, bf16[1,16,1,32,4096]{4,3,2,1,0:T(8,128)(2,1)S(1)} %copy-done.1, bf16[512,256]{1,0:T(8,128)(2,1)S(1)} %get-tuple-element.64.refs_9_.hidden_ref, bf16[512,512]{1,0:T(8,128)(2,1)S(1)} %copy-done.5, ...), custom_call_target="tpu_custom_call" | custom-call | tf_op jit(solution)/shard_map/pallas_call | solution.py:475
  (112 shorter events, 67.7 us)
Async XLA Ops:
  2.3 35.3 %collective-permute-start.14 = (bf16[3072,256]{1,0:T(8,128)(2,1)S(1)}, bf16[3072,256]{1,0:T(8,128)(2,1)S(1)}, u32[]{:S(2)}, u32[]{:S(2)}) collective-permute-start(bf16[3072,256]{1,0:T(8,128)(2,1)S(1)} %shard_map.113.refs_0_), channel_id=1, source_target_pairs={{0,4},{4,8},{8,12},{12,0},{1,5},{5,9},{9,13},{13,1},{2,6},{6,10},{... | collective-permute-start | bytes 4718600 | tf_op jit(solution)/shard_map/ppermute | solution.py:22
  4.4 41.7 %collective-permute-start.13 = (bf16[3072,256]{1,0:T(8,128)(2,1)S(1)}, bf16[3072,256]{1,0:T(8,128)(2,1)}, u32[]{:S(2)}, u32[]{:S(2)}) collective-permute-start(bf16[3072,256]{1,0:T(8,128)(2,1)S(1)} %shard_map.113.refs_0_), channel_id=1, source_target_pairs={{0,12},{4,0},{8,4},{12,8},{1,13},{5,1},{9,5},{13,9},{2,14},{6,2},{... | collective-permute-start | bytes 4718600 | tf_op jit(solution)/shard_map/ppermute | solution.py:22
  29.4 32.1 %collective-permute-start.6 = (bf16[320,1024]{1,0:T(8,128)(2,1)S(1)}, bf16[320,1024]{1,0:T(8,128)(2,1)S(1)}, u32[]{:S(2)}, u32[]{:S(2)}) collective-permute-start(bf16[320,1024]{1,0:T(8,128)(2,1)S(1)} %shard_map.111.refs_0_), channel_id=1, source_target_pairs={{0,1},{1,2},{2,3},{3,0},{4,5},{5,6},{6,7},{7,4},{8,9},{9,10},{10,1... | collective-permute-start | bytes 1966088 | tf_op jit(solution)/shard_map/ppermute | solution.py:22
  30.8 30.8 %collective-permute-start.5 = (bf16[320,1024]{1,0:T(8,128)(2,1)S(1)}, bf16[320,1024]{1,0:T(8,128)(2,1)S(1)}, u32[]{:S(2)}, u32[]{:S(2)}) collective-permute-start(bf16[320,1024]{1,0:T(8,128)(2,1)S(1)} %shard_map.111.refs_0_), channel_id=1, source_target_pairs={{0,3},{1,0},{2,1},{3,2},{4,7},{5,4},{6,5},{7,6},{8,11},{9,8},{10,9... | collective-permute-start | bytes 1966088 | tf_op jit(solution)/shard_map/ppermute | solution.py:22
  32.3 15.5 %collective-permute-start.7 = (bf16[64,1024]{1,0:T(8,128)(2,1)S(1)}, bf16[64,1024]{1,0:T(8,128)(2,1)S(1)}, u32[]{:S(2)}, u32[]{:S(2)}) collective-permute-start(bf16[64,1024]{1,0:T(8,128)(2,1)S(1)} %get-tuple-element.56), channel_id=1, source_target_pairs={{0,96},{16,112},{32,128},{48,144},{64,160},{80,176},{96,192},{112,... | collective-permute-start | bytes 393224 | tf_op jit(solution)/shard_map/ppermute | solution.py:27
  37.6 22.4 %collective-permute-start.8 = (bf16[64,1024]{1,0:T(8,128)(2,1)S(1)}, bf16[64,1024]{1,0:T(8,128)(2,1)S(1)}, u32[]{:S(2)}, u32[]{:S(2)}) collective-permute-start(bf16[64,1024]{1,0:T(8,128)(2,1)S(1)} %get-tuple-element.57), channel_id=1, source_target_pairs={{0,160},{16,176},{32,192},{48,208},{64,224},{80,240},{96,0},{112,1... | collective-permute-start | bytes 393224 | tf_op jit(solution)/shard_map/ppermute | solution.py:27
  46.1 15.4 %collective-permute-start.9 = (bf16[64,1024]{1,0:T(8,128)(2,1)S(1)}, bf16[64,1024]{1,0:T(8,128)(2,1)S(1)}, u32[]{:S(2)}, u32[]{:S(2)}) collective-permute-start(bf16[64,1024]{1,0:T(8,128)(2,1)S(1)} %get-tuple-element.58), channel_id=1, source_target_pairs={{0,128},{16,144},{32,160},{48,176},{64,192},{80,208},{96,224},{112... | collective-permute-start | bytes 393224 | tf_op jit(solution)/shard_map/ppermute | solution.py:27
  47.8 18.5 %collective-permute-start.15 = (bf16[1536,256]{1,0:T(8,128)(2,1)S(1)}, bf16[1536,256]{1,0:T(8,128)(2,1)S(1)}, u32[]{:S(2)}, u32[]{:S(2)}) collective-permute-start(bf16[1536,256]{1,0:T(8,128)(2,1)S(1)} %slice.18), channel_id=1, source_target_pairs={{0,4},{4,8},{8,12},{12,0},{1,5},{5,9},{9,13},{13,1},{2,6},{6,10},{... | collective-permute-start | bytes 2359304 | tf_op jit(solution)/shard_map/ppermute | solution.py:22
  60.0 18.0 %collective-permute-start.16 = (bf16[1536,256]{1,0:T(8,128)(2,1)S(1)}, bf16[1536,256]{1,0:T(8,128)(2,1)S(1)}, u32[]{:S(2)}, u32[]{:S(2)}) collective-permute-start(bf16[1536,256]{1,0:T(8,128)(2,1)S(1)} %slice.19), channel_id=1, source_target_pairs={{0,12},{4,0},{8,4},{12,8},{1,13},{5,1},{9,5},{13,9},{2,14},{6,2},{... | collective-permute-start | bytes 2359304 | tf_op jit(solution)/shard_map/ppermute | solution.py:22
  61.6 27.8 %collective-permute-start.10 = (bf16[352,1024]{1,0:T(8,128)(2,1)S(1)}, bf16[352,1024]{1,0:T(8,128)(2,1)S(1)}, u32[]{:S(2)}, u32[]{:S(2)}) collective-permute-start(bf16[352,1024]{1,0:T(8,128)(2,1)S(1)} %get-tuple-element.60), channel_id=1, source_target_pairs={{0,3},{1,0},{2,1},{3,2},{4,7},{5,4},{6,5},{7,6},{8,11},{9,8},{10,9... | collective-permute-start | bytes 2162696 | tf_op jit(solution)/shard_map/ppermute | solution.py:22
  64.6 24.8 %collective-permute-start.11 = (bf16[352,1024]{1,0:T(8,128)(2,1)S(1)}, bf16[352,1024]{1,0:T(8,128)(2,1)S(1)}, u32[]{:S(2)}, u32[]{:S(2)}) collective-permute-start(bf16[352,1024]{1,0:T(8,128)(2,1)S(1)} %get-tuple-element.61), channel_id=1, source_target_pairs={{0,1},{1,2},{2,3},{3,0},{4,5},{5,6},{6,7},{7,4},{8,9},{9,10},{10,1... | collective-permute-start | bytes 2162696 | tf_op jit(solution)/shard_map/ppermute | solution.py:22
  64.6 24.8 %collective-permute-start.12 = (bf16[192,1024]{1,0:T(8,128)(2,1)S(1)}, bf16[192,1024]{1,0:T(8,128)(2,1)S(1)}, u32[]{:S(2)}, u32[]{:S(2)}) collective-permute-start(bf16[192,1024]{1,0:T(8,128)(2,1)S(1)} %get-tuple-element.59.refs_3_), channel_id=1, source_target_pairs={{0,2},{1,3},{2,0},{3,1},{4,6},{5,7},{6,4},{7,5},{8,10},{9,11},{10,... | collective-permute-start | bytes 1179656 | tf_op jit(solution)/shard_map/ppermute | solution.py:22
  98.4 16.3 %collective-permute-start.36 = (bf16[1536,256]{1,0:T(8,128)(2,1)S(1)}, bf16[1536,256]{1,0:T(8,128)(2,1)S(1)}, u32[]{:S(2)}, u32[]{:S(2)}) collective-permute-start(bf16[1536,256]{1,0:T(8,128)(2,1)S(1)} %get-tuple-element.93), channel_id=1, source_target_pairs={{0,12},{4,0},{8,4},{12,8},{1,13},{5,1},{9,5},{13,9},{2,14},{6,2},{... | collective-permute-start | bytes 2359304 | tf_op jit(solution)/shard_map/ppermute | solution.py:22
  100.8 11.6 %collective-permute-start.19 = (bf16[256,1024]{1,0:T(8,128)(2,1)S(1)}, bf16[256,1024]{1,0:T(8,128)(2,1)S(1)}, u32[]{:S(2)}, u32[]{:S(2)}) collective-permute-start(bf16[256,1024]{1,0:T(8,128)(2,1)S(1)} %get-tuple-element.72), channel_id=1, source_target_pairs={{0,3},{1,0},{2,1},{3,2},{4,7},{5,4},{6,5},{7,6},{8,11},{9,8},{10,9... | collective-permute-start | bytes 1572872 | tf_op jit(solution)/shard_map/ppermute | solution.py:22
  102.2 26.7 %collective-permute-start.34 = (bf16[1536,256]{1,0:T(8,128)(2,1)S(1)}, bf16[1536,256]{1,0:T(8,128)(2,1)S(1)}, u32[]{:S(2)}, u32[]{:S(2)}) collective-permute-start(bf16[1536,256]{1,0:T(8,128)(2,1)S(1)} %get-tuple-element.91), channel_id=1, source_target_pairs={{0,4},{4,8},{8,12},{12,0},{1,5},{5,9},{9,13},{13,1},{2,6},{6,10},{... | collective-permute-start | bytes 2359304 | tf_op jit(solution)/shard_map/ppermute | solution.py:22
  111.2 23.6 %collective-permute-start.25 = (bf16[192,1024]{1,0:T(8,128)(2,1)S(1)}, bf16[192,1024]{1,0:T(8,128)(2,1)S(1)}, u32[]{:S(2)}, u32[]{:S(2)}) collective-permute-start(bf16[192,1024]{1,0:T(8,128)(2,1)S(1)} %shard_map.121), channel_id=1, source_target_pairs={{0,1},{1,2},{2,3},{3,0},{4,5},{5,6},{6,7},{7,4},{8,9},{9,10},{10,1... | collective-permute-start | bytes 1179656 | tf_op jit(solution)/shard_map/ppermute | solution.py:22
  112.6 27.6 %collective-permute-start.20 = (bf16[320,1024]{1,0:T(8,128)(2,1)S(1)}, bf16[320,1024]{1,0:T(8,128)(2,1)S(1)}, u32[]{:S(2)}, u32[]{:S(2)}) collective-permute-start(bf16[320,1024]{1,0:T(8,128)(2,1)S(1)} %shard_map.119), channel_id=1, source_target_pairs={{0,3},{1,0},{2,1},{3,2},{4,7},{5,4},{6,5},{7,6},{8,11},{9,8},{10,9... | collective-permute-start | bytes 1966088 | tf_op jit(solution)/shard_map/ppermute | solution.py:22
  114.5 25.7 %collective-permute-start.18 = (bf16[320,1024]{1,0:T(8,128)(2,1)S(1)}, bf16[320,1024]{1,0:T(8,128)(2,1)S(1)}, u32[]{:S(2)}, u32[]{:S(2)}) collective-permute-start(bf16[320,1024]{1,0:T(8,128)(2,1)S(1)} %shard_map.118), channel_id=1, source_target_pairs={{0,1},{1,2},{2,3},{3,0},{4,5},{5,6},{6,7},{7,4},{8,9},{9,10},{10,1... | collective-permute-start | bytes 1966088 | tf_op jit(solution)/shard_map/ppermute | solution.py:22
  114.8 20.0 %collective-permute-start.26 = (bf16[192,1024]{1,0:T(8,128)(2,1)S(1)}, bf16[192,1024]{1,0:T(8,128)(2,1)S(1)}, u32[]{:S(2)}, u32[]{:S(2)}) collective-permute-start(bf16[192,1024]{1,0:T(8,128)(2,1)S(1)} %shard_map.122), channel_id=1, source_target_pairs={{0,3},{1,0},{2,1},{3,2},{4,7},{5,4},{6,5},{7,6},{8,11},{9,8},{10,9... | collective-permute-start | bytes 1179656 | tf_op jit(solution)/shard_map/ppermute | solution.py:22
  128.9 64.0 %collective-permute-start.37 = (bf16[3072,256]{1,0:T(8,128)(2,1)}, bf16[3072,256]{1,0:T(8,128)(2,1)S(1)}, u32[]{:S(2)}, u32[]{:S(2)}) collective-permute-start(bf16[3072,256]{1,0:T(8,128)(2,1)} %shard_map.130), channel_id=1, source_target_pairs={{0,12},{4,0},{8,4},{12,8},{1,13},{5,1},{9,5},{13,9},{2,14},{6,2},{... | collective-permute-start | bytes 4718600 | tf_op jit(solution)/shard_map/ppermute | solution.py:22
  134.8 58.1 %collective-permute-start.35 = (bf16[3072,256]{1,0:T(8,128)(2,1)}, bf16[3072,256]{1,0:T(8,128)(2,1)}, u32[]{:S(2)}, u32[]{:S(2)}) collective-permute-start(bf16[3072,256]{1,0:T(8,128)(2,1)} %shard_map.129), channel_id=1, source_target_pairs={{0,4},{4,8},{8,12},{12,0},{1,5},{5,9},{9,13},{13,1},{2,6},{6,10},{... | collective-permute-start | bytes 4718600 | tf_op jit(solution)/shard_map/ppermute | solution.py:22
  140.3 14.0 %collective-permute-start.29 = (bf16[64,1152]{1,0:T(8,128)(2,1)S(1)}, bf16[64,1152]{1,0:T(8,128)(2,1)S(1)}, u32[]{:S(2)}, u32[]{:S(2)}) collective-permute-start(bf16[64,1152]{1,0:T(8,128)(2,1)S(1)} %get-tuple-element.84), channel_id=1, source_target_pairs={{0,128},{16,144},{32,160},{48,176},{64,192},{80,208},{96,224},{112... | collective-permute-start | bytes 442376 | tf_op jit(solution)/shard_map/ppermute | solution.py:27
  174.9 15.5 %collective-permute-start.32 = (bf16[128,1152]{1,0:T(8,128)(2,1)S(1)}, bf16[128,1152]{1,0:T(8,128)(2,1)S(1)}, u32[]{:S(2)}, u32[]{:S(2)}) collective-permute-start(bf16[128,1152]{1,0:T(8,128)(2,1)S(1)} %shard_map.125.refs_0_), channel_id=1, source_target_pairs={{0,2},{1,3},{2,0},{3,1},{4,6},{5,7},{6,4},{7,5},{8,10},{9,11},{10,... | collective-permute-start | bytes 884744 | tf_op jit(solution)/shard_map/ppermute | solution.py:22
  177.3 13.0 %collective-permute-start.31 = (bf16[128,1152]{1,0:T(8,128)(2,1)S(1)}, bf16[128,1152]{1,0:T(8,128)(2,1)S(1)}, u32[]{:S(2)}, u32[]{:S(2)}) collective-permute-start(bf16[128,1152]{1,0:T(8,128)(2,1)S(1)} %shard_map.125.refs_0_), channel_id=1, source_target_pairs={{0,3},{1,0},{2,1},{3,2},{4,7},{5,4},{6,5},{7,6},{8,11},{9,8},{10,9... | collective-permute-start | bytes 884744 | tf_op jit(solution)/shard_map/ppermute | solution.py:22
  (22 other events, 214.9 us)
